TPU v7x, 256 devices: a whole 4x4x8 slice. The times are simulated.
256 devices in a mesh: req: 32 (over x, z), mdl: 8 (over y, core).
Axes of the slice: x: 4, y: 4, z: 8, core: 2. Of those that a mesh axis runs over, the one named last changes fastest.
Arguments:
- hidden_state: bfloat16 [1024, 2880], P('req'), may hold values from -6 to 6
- cached_length_list: int32 [1024], P('req'), may hold values from 1 to 2047, as said below
- page_table: int32 [1024, 16], P('req'), may hold values from 0 to 5631, as said below
- paged_cache_store: bfloat16 [5632, 128, 1024], P('req', None, 'mdl'), may hold values from -68 to 68, as said below
- attention_gain: float32 [2880], replicated, may hold values from 0.5 to 1.5
- qkv_weight: bfloat16 [2880, 5120], P('req', 'mdl'), may hold values from -0.109375 to 0.109375
- qkv_bias: float32 [5120], P('mdl'), may hold values from -3 to 3
- sink_logit_values: float32 [64], P('mdl'), may hold values from -1 to 4
- output_weight: bfloat16 [4096, 2880], P('mdl', 'req'), may hold values from -0.25 to 0.25
- output_bias: float32 [2880], replicated, may hold values from -3 to 3
- expert_gain: float32 [2880], replicated, may hold values from 0.5 to 1.5
- router_weight: bfloat16 [2880, 32], replicated, may hold values from -0.109375 to 0.109375
- router_bias: float32 [32], replicated, may hold values from -4 to 4
- expert_routes: int32 [1024, 4], P('req'), may hold values from 0 to 31, all different within a row; in each aligned block of 32 rows (0 to 31, 32 to 63, ...) at most 8 rows name the same one
- expand_weight: bfloat16 [32, 2880, 5760], P('req', None, 'mdl'), may hold values from -0.109375 to 0.109375
- expand_bias: float32 [32, 5760], P('req', 'mdl'), may hold values from -10 to 10
- reduce_weight: bfloat16 [32, 2880, 2880], P('req', 'mdl'), may hold values from -0.109375 to 0.109375
- reduce_bias: float32 [32, 2880], replicated, may hold values from -3 to 3
Outputs:
- layer_output: bfloat16 [1024, 2880], P('req', 'mdl')
Inputs may be any that keep to these rules, and one draw needn't show every extreme that they name: `cached_length_list`: requests r and r + 1 within a block of 32 requests share an owner; about one request in eight holds between 1536 and 2047 cached positions, at most 8 of each owner's 32, and the others at most 256; some owner, and the last owner, hold exactly 8 long ones. `page_table`: the entries of request r name pages of its owner's block, pages r // 32 * 176 to that plus 176 - 1; the pages that hold cached positions differ between requests; entries past a request's last used page are to be ignored. `paged_cache_store`: keys are stored rotated at their own positions. `expert_routes`: each token names 4 different experts; of the rows of one index of req no expert is named by more than 8.
All inputs are finite; a program needn't handle non-finite values.
Results may differ from a plain program's by a relative error of at most 0.024.
Values may be sent and summed in bfloat16 or wider, within the bound.
A program may use at most 192 MiB of HBM per device.

v0:
```python
import math
import jax
import jax.numpy as jnp
from jax import lax
from jax.sharding import PartitionSpec as P

HEAD_SIZE = 64
PAGE_POSITIONS = 128
SHORT_MAX = 256
QUERY_PER_KEY = 8
SHORT_PAGES = 2
norm_epsilon = 1e-05
rope_theta = 150000.0
swiglu_limit = 7.0
swiglu_alpha = 1.702


def normalize(row_values, gain):
    value_rows = row_values.astype(jnp.float32)
    mean_square = jnp.mean(value_rows * value_rows, axis=-1, keepdims=True)
    return value_rows * lax.rsqrt(mean_square + norm_epsilon) * gain


def apply_rotation(value_rows, positions):
    half_width = value_rows.shape[-1] // 2
    exponent = jnp.arange(half_width, dtype=jnp.float32) * (2.0 / value_rows.shape[-1])
    frequency = jnp.power(rope_theta, -exponent)
    angles = positions.astype(jnp.float32)[:, None] * frequency[None, :]
    cosine = jnp.cos(angles)[:, None, :]
    sine_part = jnp.sin(angles)[:, None, :]
    first_half = value_rows[..., :half_width]
    second_half = value_rows[..., half_width:]
    return jnp.concatenate(
        [
            first_half * cosine - second_half * sine_part,
            second_half * cosine + first_half * sine_part,
        ],
        axis=-1,
    )


def head_identity(kv_heads):
    return (jnp.arange(kv_heads)[:, None] == jnp.arange(kv_heads)[None, :]).astype(jnp.float32)


def spread_queries(query_rows):
    row_count, kv_heads, group_size, head_width = query_rows.shape
    key_slot = (jnp.arange(2) == 0).astype(jnp.float32)
    turned = jnp.swapaxes(query_rows, 2, 3).astype(jnp.float32)
    spread = jnp.einsum("rhdg,kh,s->rksdhg", turned, head_identity(kv_heads), key_slot)
    return spread.astype(jnp.bfloat16).reshape(
        row_count, kv_heads * 2 * head_width, kv_heads * group_size
    )


def part_scores(query_block, table, first_position, lengths, cache_page_store, head_width):
    row_count = query_block.shape[0]
    cached_entries = cache_page_store[table].reshape(row_count, -1, cache_page_store.shape[-1])
    score_scale = 1.0 / math.sqrt(head_width)
    scores = (
        jnp.einsum("rlc,rcq->rql", cached_entries, query_block, preferred_element_type=jnp.float32)
        * score_scale
    )
    positions = first_position + jnp.arange(scores.shape[-1])
    is_live = positions[None, :] < lengths[:, None]
    scores = jnp.where(is_live[:, None, :], scores, -jnp.inf)
    return (cached_entries, scores)


def attend_cache(
    query_rows, new_keys, new_values, lengths, local_table, cache_page_store, sink_logits
):
    row_count, kv_heads, group_size, head_width = query_rows.shape
    score_scale = 1.0 / math.sqrt(head_width)
    query_block = spread_queries(query_rows)
    short_cached, short_scores = part_scores(
        query_block, local_table[:, :SHORT_PAGES], 0, lengths, cache_page_store, head_width
    )
    long_count = row_count // 4
    is_long = lengths > SHORT_MAX
    long_rows = jnp.nonzero(is_long, size=long_count, fill_value=0)[0].astype(jnp.int32)
    long_valid = jnp.arange(long_count) < jnp.sum(is_long.astype(jnp.int32))
    long_lengths = jnp.where(long_valid, lengths[long_rows], 0)
    long_cached, long_scores = part_scores(
        query_block[long_rows],
        local_table[long_rows, SHORT_PAGES:],
        SHORT_PAGES * PAGE_POSITIONS,
        long_lengths,
        cache_page_store,
        head_width,
    )
    own_score = (
        jnp.einsum(
            "rhgd,rhd->rhg", query_rows, new_keys, preferred_element_type=jnp.float32
        ).reshape(row_count, -1)
        * score_scale
    )
    largest = jnp.maximum(jnp.maximum(jnp.max(short_scores, axis=-1), own_score), sink_logits[None])
    largest = largest.at[long_rows].max(jnp.max(long_scores, axis=-1))
    long_largest = largest[long_rows]
    short_weight = jnp.exp(short_scores - largest[..., None])
    long_weight = jnp.exp(long_scores - long_largest[..., None])
    own_weight = jnp.exp(own_score - largest)
    denominator = jnp.sum(short_weight, axis=-1) + own_weight + jnp.exp(sink_logits[None] - largest)
    denominator = denominator.at[long_rows].add(jnp.sum(long_weight, axis=-1))
    long_denominator = denominator[long_rows]
    short_share = (short_weight / denominator[..., None]).astype(jnp.bfloat16)
    long_share = (long_weight / long_denominator[..., None]).astype(jnp.bfloat16)
    own_share = (own_weight / denominator).astype(jnp.bfloat16)
    wide_mixture = jnp.einsum(
        "rql,rlc->rqc", short_share, short_cached, preferred_element_type=jnp.float32
    )
    long_mixture = jnp.einsum(
        "rql,rlc->rqc", long_share, long_cached, preferred_element_type=jnp.float32
    )
    wide_mixture = wide_mixture.at[long_rows].add(long_mixture)
    wide_mixture = wide_mixture.reshape(row_count, kv_heads, group_size, kv_heads, 2, head_width)
    value_slot = (jnp.arange(2) == 1).astype(jnp.float32)
    mixture = jnp.einsum("rhgksd,hk,s->rhgd", wide_mixture, head_identity(kv_heads), value_slot)
    own_part = own_share.astype(jnp.float32).reshape(row_count, kv_heads, group_size)
    mixture = mixture + own_part[..., None] * new_values.astype(jnp.float32)[:, :, None, :]
    return mixture.astype(jnp.bfloat16).reshape(row_count, -1)


def expert_block(received, expand_local, expand_local_bias, reduce_local):
    sources, item_count, model_width = received.shape
    flattened = received.reshape(sources * item_count, model_width)
    pre_activation = (
        jnp.dot(flattened, expand_local, preferred_element_type=jnp.float32) + expand_local_bias
    )
    gate_part = jnp.minimum(pre_activation[:, 0::2], swiglu_limit)
    up_part = jnp.clip(pre_activation[:, 1::2], -swiglu_limit, swiglu_limit)
    activation = (gate_part * jax.nn.sigmoid(swiglu_alpha * gate_part) * (up_part + 1.0)).astype(
        jnp.bfloat16
    )
    return jnp.dot(activation, reduce_local, preferred_element_type=jnp.float32).reshape(
        sources, item_count, -1
    )


def shards(
    hidden_state,
    cached_length_list,
    page_table,
    paged_cache_store,
    attention_gain,
    qkv_weight,
    qkv_bias,
    sink_logit_values,
    output_weight,
    output_bias,
    expert_gain,
    router_weight,
    router_bias,
    expert_routes,
    expand_weight,
    expand_bias,
    reduce_weight,
    reduce_bias,
):
    rows_here, model_width = hidden_state.shape
    normed = normalize(hidden_state, attention_gain).astype(jnp.bfloat16)
    qkv_full, output_full = (
        lax.all_gather(qkv_weight, "req", axis=0, tiled=True),
        lax.all_gather(output_weight, "req", axis=1, tiled=True),
    )
    projected_rows = jnp.dot(normed, qkv_full, preferred_element_type=jnp.float32)
    projected_rows = (projected_rows + qkv_bias).reshape(
        rows_here, -1, QUERY_PER_KEY + 2, HEAD_SIZE
    )
    kv_heads = projected_rows.shape[1]
    query_rows = (
        apply_rotation(
            projected_rows[:, :, :QUERY_PER_KEY].reshape(
                rows_here, kv_heads * QUERY_PER_KEY, HEAD_SIZE
            ),
            cached_length_list,
        )
        .astype(jnp.bfloat16)
        .reshape(rows_here, kv_heads, QUERY_PER_KEY, HEAD_SIZE)
    )
    new_keys = apply_rotation(projected_rows[:, :, QUERY_PER_KEY], cached_length_list).astype(
        jnp.bfloat16
    )
    new_values = projected_rows[:, :, QUERY_PER_KEY + 1].astype(jnp.bfloat16)
    local_table = page_table - lax.axis_index("req") * paged_cache_store.shape[0]
    attended = attend_cache(
        query_rows,
        new_keys,
        new_values,
        cached_length_list,
        local_table,
        paged_cache_store,
        sink_logit_values,
    )
    partial_value = jnp.dot(attended, output_full, preferred_element_type=jnp.float32)
    head_total = lax.psum(partial_value.astype(jnp.bfloat16), "mdl").astype(jnp.float32)
    residual = (hidden_state.astype(jnp.float32) + head_total + output_bias).astype(jnp.bfloat16)
    expert_input = normalize(residual, expert_gain).astype(jnp.bfloat16)
    logits = jnp.dot(expert_input, router_weight, preferred_element_type=jnp.float32) + router_bias
    experts = router_weight.shape[1]
    route_count = expert_routes.shape[1]
    one_hot = expert_routes[:, :, None] == jnp.arange(experts)[None, None, :]
    chosen = jnp.sum(jnp.where(one_hot, logits[:, None, :], 0.0), axis=-1)
    gate_weights = jax.nn.softmax(chosen, axis=-1)
    capacity = max(2, 2 * rows_here * route_count // experts)
    pair_hot = one_hot.reshape(rows_here * route_count, experts).astype(jnp.int32)
    counts_before = jnp.cumsum(pair_hot, axis=0) - pair_hot
    slot_index = jnp.sum(counts_before * pair_hot, axis=1)
    target = expert_routes.reshape(-1) * capacity + slot_index
    placement = target[:, None] == jnp.arange(experts * capacity)[None, :]
    repeated = jnp.repeat(expert_input, route_count, axis=0)
    outgoing = jnp.einsum(
        "pc,pd->cd", placement.astype(jnp.bfloat16), repeated, preferred_element_type=jnp.float32
    )
    outgoing = outgoing.astype(jnp.bfloat16).reshape(experts, capacity, model_width)
    results = expert_block(
        lax.all_to_all(outgoing, "req", split_axis=0, concat_axis=0, tiled=True),
        expand_weight[0],
        expand_bias[0],
        reduce_weight[0],
    )
    share_width = model_width // lax.axis_size("mdl")
    offset = lax.axis_index("mdl") * share_width
    shares = lax.psum_scatter(
        results.astype(jnp.bfloat16), "mdl", scatter_dimension=2, tiled=True
    ).astype(jnp.float32)
    returned = lax.all_to_all(
        shares.astype(jnp.bfloat16), "req", split_axis=0, concat_axis=0, tiled=True
    ).astype(shares.dtype)
    picked = returned.reshape(-1, share_width)[target]
    blended = jnp.sum(
        picked.reshape(rows_here, route_count, share_width) * gate_weights[:, :, None], axis=1
    )
    bias_rows = lax.dynamic_slice_in_dim(reduce_bias, offset, share_width, 1)
    bias_term = jnp.sum(bias_rows[expert_routes] * gate_weights[:, :, None], axis=1)
    residual_share = lax.dynamic_slice_in_dim(residual, offset, share_width, 1).astype(jnp.float32)
    return (residual_share + blended + bias_term).astype(jnp.bfloat16)


def solution(mesh):
    in_specs = (
        P("req", None),
        P("req"),
        P("req", None),
        P("req", None, "mdl"),
        P(),
        P("req", "mdl"),
        P("mdl"),
        P("mdl"),
        P("mdl", "req"),
        P(),
        P(),
        P(),
        P(),
        P("req", None),
        P("req", None, "mdl"),
        P("req", "mdl"),
        P("req", "mdl", None),
        P(),
    )
    out_specs = P("req", "mdl")
    return jax.shard_map(shards, mesh=mesh, in_specs=in_specs, out_specs=out_specs, check_vma=False)
```

profile of v0, /device:TPU:32, one launch (start us, length us, event | category | flops | bytes accessed | tf_op | source)
XLA Modules:
  0.0 452.2 jit_solution(11918151416933086248)
XLA Ops:
  6.5 0.7 all-gather.7.cloned.1.call-update
  9.9 0.8 scatter_custom_fusion
  10.9 1.4 fusion.56
  12.9 1.3 gather_fusion.1
  14.9 16.5 %while.1 = (s32[]{:T(128)}, s32[32,16]{0,1:T(8,128)S(1)}, s32[8,2]{0,1:T(2,128)S(1)}, s32[8,14]{1,0:T(8,128)S(1)}, s32[]{:T(128)}, /*index=5*/s32[]{:T(128)}) while((s32[]{:T(128)}, s32[32,16]{0,1:T(8,128)S(1)}, s32[8,2]{0,1:T(2,128)S(1)}, s32[8,14]{1,0:T(8,128)S(1)}, s32[]{:T(128)}, /*index=5*/s32[]{:T(128)}) %tuple.28), condition=%wide.while_cond, body=%wide.while_body.sunk | while | flops 2 | bytes 449 | solution.py:86
  15.5 1.3 dynamic-slice.7
  17.6 1.3 dynamic-slice.7
  19.6 1.3 dynamic-slice.7
  21.7 1.3 dynamic-slice.7
  23.8 1.3 dynamic-slice.7
  25.8 1.3 dynamic-slice.7
  27.9 1.3 dynamic-slice.7
  30.0 1.3 dynamic-slice.7
  31.5 4.8 %gather_fusion = bf16[64,128,128]{2,1,0:T(8,128)(2,1)} fusion(bf16[176,128,128]{2,1,0:T(8,128)(2,1)} %param.21, s32[1024]{0:T(1024)S(1)} %pad_clamp_fusion.4), kind=kCustom, calls=%fused_computation | custom fusion | bytes 4194560 | tf_op jit(solution)/shard_map/gather | solution.py:58
  36.3 5.7 %gather_fusion.3 = bf16[112,128,128]{2,1,0:T(8,128)(2,1)} fusion(bf16[176,128,128]{2,1,0:T(8,128)(2,1)} %param.21, s32[1024]{0:T(1024)S(1)} %pad_clamp_fusion.2), kind=kCustom, calls=%fused_computation.3 | custom fusion | bytes 7340480 | tf_op jit(solution)/shard_map/gather | solution.py:58
  43.8 47.9 %all-gather.7.cloned.1.call-done = bf16[32,90,512]{2,1,0:T(8,128)(2,1)} async-done(((bf16[1,90,512]{2,1,0:T(8,128)(2,1)}), bf16[32,90,512]{2,1,0:T(8,128)(2,1)}) %all-gather.7.cloned.1.call-update) | async-done | bytes 2949136 | tf_op jit(solution)/shard_map/all_gather | solution.py:165
  91.7 4.4 reshape.625
  96.1 76.7 %all-gather.5.cloned.1.call-done = bf16[32,90,640]{2,1,0:T(8,128)(2,1)} async-done(((bf16[1,90,640]{2,1,0:T(8,128)(2,1)}), bf16[32,90,640]{2,1,0:T(8,128)(2,1)}) %all-gather.5.cloned.1.call-update) | async-done | bytes 3686416 | tf_op jit(solution)/shard_map/all_gather | solution.py:164
  172.9 4.9 %reshape.623 = bf16[2880,640]{1,0:T(8,128)(2,1)} reshape(bf16[32,90,640]{2,1,0:T(8,128)(2,1)} %all-gather.5.cloned.1.call-done) | data formatting | bytes 7372800
  177.7 2.8 convolution_add_fusion
  182.2 2.3 fusion.64
  184.6 3.2 fusion.65
  190.6 2.0 fusion.29
  192.7 2.7 fusion.21
  195.4 0.8 scatter_fusion.2
  196.8 3.5 convolution_convert_fusion.2
  200.3 62.1 %all-reduce.3.cloned.1.call-done = bf16[32,2880]{1,0:T(8,128)(2,1)} async-done(((bf16[32,2880]{1,0:T(8,128)(2,1)}), bf16[32,2880]{1,0:T(8,128)(2,1)}) %all-reduce.3.cloned.1.call-update) | async-done | bytes 184336 | tf_op jit(solution)/shard_map/psum | solution.py:197
  262.4 1.1 fusion.12
  263.6 1.1 broadcast_in_dim.57
  264.7 1.6 reshape.490
  266.3 1.8 convolution_convert_fusion.1
  268.1 2.6 copy.49
  270.6 10.1 %all-to-all-start = ((bf16[32,8,2880]{2,1,0:T(8,128)(2,1)}), bf16[32,8,2880]{2,1,0:T(8,128)(2,1)}, u32[]{:S(2)}, u32[]{:S(2)}) async-start(bf16[32,8,2880]{2,1,0:T(8,128)(2,1)} %bitcast.100), calls=%async_computation | async-start | bytes 3014656 | tf_op jit(solution)/shard_map/all_to_all | solution.py:218
  281.0 35.4 %all-to-all-done = bf16[32,8,2880]{2,1,0:T(8,128)(2,1)} async-done(((bf16[32,8,2880]{2,1,0:T(8,128)(2,1)}), bf16[32,8,2880]{2,1,0:T(8,128)(2,1)}, u32[]{:S(2)}, u32[]{:S(2)}) %all-to-all-start) | async-done | bytes 1474592 | tf_op jit(solution)/shard_map/all_to_all | solution.py:218
  316.4 4.9 %fusion.5 = f32[256,720]{0,1:T(8,128)} fusion(bf16[1,2880,720]{1,2,0:T(8,128)(2,1)} %param.32, bf16[32,8,2880]{2,1,0:T(8,128)(2,1)} %all-to-all-done, f32[720]{0:T(1024)S(1)} %reduce.1), kind=kOutput, calls=%fused_computation.22 | convolution fusion | flops 1061867520 | bytes 6361920 | tf_op jit(solution)/shard_map/dot_general | solution.py:129
  321.3 2.1 slice.39
  323.4 2.1 slice.40
  325.8 2.1 convolution_convert_fusion
  327.8 20.3 %copy.58 = bf16[32,8,2880]{1,0,2:T(8,128)(2,1)} copy(bf16[32,8,2880]{2,1,0:T(8,128)(2,1)} %convolution_convert_fusion) | data formatting | bytes 2949120
  348.2 32.7 %reshape.631 = bf16[2880,256]{1,0:T(8,128)(2,1)} reshape(bf16[2880,32,8]{2,1,0:T(8,128)(2,1)} %bitcast.94) | data formatting | bytes 2949120
  381.4 0.9 constant_dynamic-slice_fusion.1
  382.3 0.8 gather_fusion.7
  383.4 30.0 %reduce-scatter.4.cloned.1.call-done = bf16[360,256]{1,0:T(8,128)(2,1)} async-done(((bf16[2880,256]{1,0:T(8,128)(2,1)}), bf16[360,256]{1,0:T(8,128)(2,1)}) %reduce-scatter.4.cloned.1.call-update) | async-done | bytes 184336
  413.4 5.4 %reshape.632 = bf16[360,32,8]{2,1,0:T(8,128)(2,1)} reshape(bf16[360,256]{1,0:T(8,128)(2,1)} %reduce-scatter.4.cloned.1.call-done) | data formatting | bytes 368640
  418.8 4.5 copy.59
  423.3 10.0 %all-to-all-start.1 = ((bf16[32,8,360]{2,1,0:T(8,128)(2,1)}), bf16[32,8,360]{2,1,0:T(8,128)(2,1)S(1)}, u32[]{:S(2)}, u32[]{:S(2)}) async-start(bf16[32,8,360]{2,1,0:T(8,128)(2,1)} %copy.59), calls=%async_computation.1 | async-start | bytes 393216 | tf_op jit(solution)/shard_map/all_to_all | solution.py:228
  433.6 10.2 %all-to-all-done.1 = bf16[32,8,360]{2,1,0:T(8,128)(2,1)S(1)} async-done(((bf16[32,8,360]{2,1,0:T(8,128)(2,1)}), bf16[32,8,360]{2,1,0:T(8,128)(2,1)S(1)}, u32[]{:S(2)}, u32[]{:S(2)}) %all-to-all-start.1) | async-done | bytes 184352 | tf_op jit(solution)/shard_map/all_to_all | solution.py:228
  443.8 0.8 gather_fusion.6
  (148 shorter events, 19.8 us)
Async XLA Ops:
  6.5 319.2 %copy-start = (bf16[1,360,2880]{2,1,0:T(8,128)(2,1)S(1)}, bf16[1,360,2880]{2,1,0:T(8,128)(2,1)}, u32[]{:S(2)}) copy-start(bf16[1,360,2880]{2,1,0:T(8,128)(2,1)} %param.34) | copy-start | bytes 6220804
  6.5 85.2 %all-gather.7.cloned.1.call-start = ((), (), s32[]{:S(2)}) async-start(), calls=%async_computation.5 | async-start | bytes 3244032 | tf_op jit(solution)/shard_map/all_gather | solution.py:165
  7.3 165.6 %all-gather.5.cloned.1.call-start = ((), (), s32[]{:S(2)}) async-start(), calls=%async_computation.4 | async-start | bytes 4055040 | tf_op jit(solution)/shard_map/all_gather | solution.py:164
  8.0 254.4 %all-reduce.3.cloned.1.call-start = ((), (), s32[]{:S(2)}) async-start(), calls=%async_computation.3 | async-start | bytes 376832 | tf_op jit(solution)/shard_map/psum | solution.py:197
  36.3 5.7 %copy-start.5 = (s32[32,4]{0,1:T(4,128)S(1)}, s32[32,4]{0,1:T(4,128)}, u32[]{:S(2)}) copy-start(s32[32,4]{0,1:T(4,128)} %param.31) | copy-start | bytes 1540
  36.3 6.4 %copy-start.3 = (bf16[32,2880]{1,0:T(8,128)(2,1)S(1)}, bf16[32,2880]{1,0:T(8,128)(2,1)}, u32[]{:S(2)}) copy-start(bf16[32,2880]{1,0:T(8,128)(2,1)} %param.18) | copy-start | bytes 552964
  36.3 7.2 %copy-start.2 = (s32[32]{0:T(128)S(1)}, s32[32]{0:T(128)}, u32[]{:S(2)}) copy-start(s32[32]{0:T(128)} %param.19) | copy-start | bytes 388
  96.1 81.6 %copy-start.8 = (f32[2880]{0:T(1024)S(1)}, f32[2880]{0:T(1024)}, u32[]{:S(2)}) copy-start(f32[2880]{0:T(1024)} %param.22) | copy-start | bytes 34564
  96.1 81.6 %copy-start.9 = (f32[640]{0:T(1024)S(1)}, f32[640]{0:T(1024)}, u32[]{:S(2)}) copy-start(f32[640]{0:T(1024)} %param.24) | copy-start | bytes 7684
  180.6 4.0 copy-start.11
  195.4 67.0 %copy-start.7 = (f32[2880]{0:T(1024)S(1)}, f32[2880]{0:T(1024)}, u32[]{:S(2)}) copy-start(f32[2880]{0:T(1024)} %param.27) | copy-start | bytes 34564
  195.4 68.1 %copy-start.6 = (f32[2880]{0:T(1024)S(1)}, f32[2880]{0:T(1024)}, u32[]{:S(2)}) copy-start(f32[2880]{0:T(1024)} %param.28) | copy-start | bytes 34564
  268.1 12.9 %copy-start.10 = (f32[1,720]{1,0:T(1,128)S(1)}, f32[1,720]{1,0:T(1,128)}, u32[]{:S(2)}) copy-start(f32[1,720]{1,0:T(1,128)} %param.33) | copy-start | bytes 8644
  270.6 45.8 %all-to-all-start = ((bf16[32,8,2880]{2,1,0:T(8,128)(2,1)}), bf16[32,8,2880]{2,1,0:T(8,128)(2,1)}, u32[]{:S(2)}, u32[]{:S(2)}) async-start(bf16[32,8,2880]{2,1,0:T(8,128)(2,1)} %bitcast.100), calls=%async_computation | async-start | bytes 3014656 | tf_op jit(solution)/shard_map/all_to_all | solution.py:218
  280.7 132.7 %reduce-scatter.4.cloned.1.call-start = ((), (), s32[]{:S(2)}) async-start(), calls=%async_computation.6 | async-start | bytes 1658880
  380.9 2.2 copy-start.4
  380.9 2.2 copy-start.12
  418.8 26.9 %copy-start.1 = (bf16[1,360,2880]{2,1,0:T(8,128)(2,1)S(1)}, bf16[1,360,2880]{2,1,0:T(8,128)(2,1)}, u32[]{:S(2)}) copy-start(bf16[1,360,2880]{2,1,0:T(8,128)(2,1)} %param.34) | copy-start | bytes 6220804
  423.3 20.5 %all-to-all-start.1 = ((bf16[32,8,360]{2,1,0:T(8,128)(2,1)}), bf16[32,8,360]{2,1,0:T(8,128)(2,1)S(1)}, u32[]{:S(2)}, u32[]{:S(2)}) async-start(bf16[32,8,360]{2,1,0:T(8,128)(2,1)} %copy.59), calls=%async_computation.1 | async-start | bytes 393216 | tf_op jit(solution)/shard_map/all_to_all | solution.py:228
Sparse Core Ops, SparseCore 0:
  9.9 81.7 all-gather.6
  94.3 78.5 all-gather.4
  200.4 61.9 all-reduce.2
  381.1 32.2 reduce-scatter.3
where the time goes:
time: 454 us; the launch traced here: 452 us
  waiting for transfers between devices  264 us (58%)
  local copies, waits for them, and re-layouts  116 us (26%)
  matrix products  25.9 us (6%)
  starting transfers between devices  20.4 us (4%)
  between operations  13.7 us (3%)
  other arithmetic  12.6 us (3%)
    all_gather x1, waiting for transfers between devices, shards(): lax.all_gather(qkv_weight, 'req', axis=0, tiled=True)  76.7 us
    unnamed x33, local copies, waits for them, and re-layouts  72.4 us
    psum x1, waiting for transfers between devices, shards(): lax.psum(partial_value.astype(jnp.bfloat16), 'mdl').astype(jnp.float32)  62.1 us
    all_gather x1, waiting for transfers between devices, shards(): lax.all_gather(output_weight, 'req', axis=1, tiled=True)  47.9 us
    all_to_all x1, waiting for transfers between devices, shards(): lax.all_to_all(outgoing, 'req', split_axis=0, concat_axis=0, tiled=True)  35.4 us
    unnamed x5, waiting for transfers between devices  31.5 us
    gather x40, local copies, waits for them, and re-layouts  16.5 us
    gather x2, local copies, waits for them, and re-layouts, part_scores(): cache_page_store[table].reshape(row_count, -1, cache_page_store.shape[-1])  10.5 us
  transfers between devices with their start and end apart: 6, of which 6 were waited for; matrix products, arithmetic and copies ran while one was open for 9% of the time, Pallas kernels for 0%

commit v1 on v0

--- a/solution.py
+++ b/solution.py
@@ -194,7 +194,9 @@
         sink_logit_values,
     )
     partial_value = jnp.dot(attended, output_full, preferred_element_type=jnp.float32)
-    head_total = lax.psum(partial_value.astype(jnp.bfloat16), "mdl").astype(jnp.float32)
+    head_total = jnp.sum(lax.all_gather(partial_value.astype(jnp.bfloat16), "mdl"), axis=0).astype(
+        jnp.float32
+    )
     residual = (hidden_state.astype(jnp.float32) + head_total + output_bias).astype(jnp.bfloat16)
     expert_input = normalize(residual, expert_gain).astype(jnp.bfloat16)
     logits = jnp.dot(expert_input, router_weight, preferred_element_type=jnp.float32) + router_bias

time: 454 us -> 419 us (0.923)
  waiting for transfers between devices: 264 us -> 227 us
    psum x1 -> x0, waiting for transfers between devices: 62.1 us -> none  [shards(): lax.psum(partial_value.astype(jnp.bfloat16), 'mdl').astype(jnp.float32)]
    all_gather x0 -> x1, waiting for transfers between devices: none -> 23.6 us  [shards(): lax.all_gather(partial_value.astype(jnp.bfloat16), 'mdl')]
  transfers between devices with their start and end apart: 6 -> 6, of which waited for: 6 -> 6; matrix products, arithmetic and copies ran while one was open for 9% -> 10% of each run, Pallas kernels for 0% -> 0%
where the time goes in v1:
time: 419 us; the launch traced here: 416 us
  waiting for transfers between devices  227 us (54%)
  local copies, waits for them, and re-layouts  116 us (28%)
  matrix products  25.9 us (6%)
  starting transfers between devices  20.5 us (5%)
  between operations  13.7 us (3%)
  other arithmetic  13.4 us (3%)
    all_gather x1, waiting for transfers between devices, shards(): lax.all_gather(qkv_weight, 'req', axis=0, tiled=True)  76.7 us
    unnamed x33, local copies, waits for them, and re-layouts  72.4 us
    all_gather x1, waiting for transfers between devices, shards(): lax.all_gather(output_weight, 'req', axis=1, tiled=True)  48.6 us
    all_to_all x1, waiting for transfers between devices, shards(): lax.all_to_all(outgoing, 'req', split_axis=0, concat_axis=0, tiled=True)  37.6 us
    unnamed x5, waiting for transfers between devices  30.6 us
    all_gather x1, waiting for transfers between devices, shards(): lax.all_gather(partial_value.astype(jnp.bfloat16), 'mdl')  23.6 us
    gather x40, local copies, waits for them, and re-layouts  16.5 us
    gather x2, local copies, waits for them, and re-layouts, part_scores(): cache_page_store[table].reshape(row_count, -1, cache_page_store.shape[-1])  10.5 us
  transfers between devices with their start and end apart: 6, of which 6 were waited for; matrix products, arithmetic and copies ran while one was open for 10% of the time, Pallas kernels for 0%

profile of v1, /device:TPU:32, one launch (start us, length us, event | category | flops | bytes accessed | tf_op | source)
XLA Modules:
  0.0 416.5 jit_solution(4213437509069546986)
XLA Ops:
  6.5 0.7 all-gather.11.cloned.1.call-update
  9.9 0.8 scatter_custom_fusion
  10.9 1.4 fusion.56
  12.9 1.3 gather_fusion.1
  14.9 16.5 %while.1 = (s32[]{:T(128)}, s32[32,16]{0,1:T(8,128)S(1)}, s32[8,2]{0,1:T(2,128)S(1)}, s32[8,14]{1,0:T(8,128)S(1)}, s32[]{:T(128)}, /*index=5*/s32[]{:T(128)}) while((s32[]{:T(128)}, s32[32,16]{0,1:T(8,128)S(1)}, s32[8,2]{0,1:T(2,128)S(1)}, s32[8,14]{1,0:T(8,128)S(1)}, s32[]{:T(128)}, /*index=5*/s32[]{:T(128)}) %tuple.28), condition=%wide.while_cond, body=%wide.while_body.sunk | while | flops 2 | bytes 449 | solution.py:86
  15.5 1.3 dynamic-slice.7
  17.6 1.3 dynamic-slice.7
  19.6 1.3 dynamic-slice.7
  21.7 1.3 dynamic-slice.7
  23.8 1.3 dynamic-slice.7
  25.8 1.3 dynamic-slice.7
  27.9 1.3 dynamic-slice.7
  30.0 1.3 dynamic-slice.7
  31.5 4.8 %gather_fusion = bf16[64,128,128]{2,1,0:T(8,128)(2,1)} fusion(bf16[176,128,128]{2,1,0:T(8,128)(2,1)} %param.21, s32[1024]{0:T(1024)S(1)} %pad_clamp_fusion.4), kind=kCustom, calls=%fused_computation | custom fusion | bytes 4194560 | tf_op jit(solution)/shard_map/gather | solution.py:58
  36.3 5.7 %gather_fusion.3 = bf16[112,128,128]{2,1,0:T(8,128)(2,1)} fusion(bf16[176,128,128]{2,1,0:T(8,128)(2,1)} %param.21, s32[1024]{0:T(1024)S(1)} %pad_clamp_fusion.2), kind=kCustom, calls=%fused_computation.3 | custom fusion | bytes 7340480 | tf_op jit(solution)/shard_map/gather | solution.py:58
  43.2 48.6 %all-gather.11.cloned.1.call-done = bf16[32,90,512]{2,1,0:T(8,128)(2,1)} async-done(((bf16[1,90,512]{2,1,0:T(8,128)(2,1)}), bf16[32,90,512]{2,1,0:T(8,128)(2,1)}) %all-gather.11.cloned.1.call-update) | async-done | bytes 2949136 | tf_op jit(solution)/shard_map/all_gather | solution.py:165
  91.7 4.4 %reshape.626 = bf16[2880,512]{1,0:T(8,128)(2,1)} reshape(bf16[32,90,512]{2,1,0:T(8,128)(2,1)} %all-gather.11.cloned.1.call-done) | data formatting | bytes 5898240
  96.1 76.7 %all-gather.9.cloned.1.call-done = bf16[32,90,640]{2,1,0:T(8,128)(2,1)} async-done(((bf16[1,90,640]{2,1,0:T(8,128)(2,1)}), bf16[32,90,640]{2,1,0:T(8,128)(2,1)}) %all-gather.9.cloned.1.call-update) | async-done | bytes 3686416 | tf_op jit(solution)/shard_map/all_gather | solution.py:164
  172.9 4.9 %reshape.624 = bf16[2880,640]{1,0:T(8,128)(2,1)} reshape(bf16[32,90,640]{2,1,0:T(8,128)(2,1)} %all-gather.9.cloned.1.call-done) | data formatting | bytes 7372800
  177.7 2.8 convolution_add_fusion
  182.2 2.3 fusion.64
  184.6 3.2 fusion.65
  190.6 2.0 fusion.29
  192.7 2.7 fusion.21
  195.4 0.8 scatter_fusion.2
  196.8 3.5 convolution_convert_fusion.2
  201.0 23.6 %all-gather.7.cloned.1.call-done = bf16[256,2880]{1,0:T(8,128)(2,1)} async-done(((bf16[32,2880]{1,0:T(8,128)(2,1)}), bf16[256,2880]{1,0:T(8,128)(2,1)}) %all-gather.7.cloned.1.call-update) | async-done | bytes 1474576 | tf_op jit(solution)/shard_map/all_gather | solution.py:197
  224.5 1.6 reduce_sum.112
  226.5 1.1 broadcast_in_dim.57
  227.6 1.6 reshape.490
  229.2 1.8 convolution_convert_fusion.1
  230.9 2.6 copy.49
  233.5 10.1 %all-to-all-start = ((bf16[32,8,2880]{2,1,0:T(8,128)(2,1)}), bf16[32,8,2880]{2,1,0:T(8,128)(2,1)}, u32[]{:S(2)}, u32[]{:S(2)}) async-start(bf16[32,8,2880]{2,1,0:T(8,128)(2,1)} %bitcast.101), calls=%async_computation | async-start | bytes 3014656 | tf_op jit(solution)/shard_map/all_to_all | solution.py:220
  243.8 37.6 %all-to-all-done = bf16[32,8,2880]{2,1,0:T(8,128)(2,1)} async-done(((bf16[32,8,2880]{2,1,0:T(8,128)(2,1)}), bf16[32,8,2880]{2,1,0:T(8,128)(2,1)}, u32[]{:S(2)}, u32[]{:S(2)}) %all-to-all-start) | async-done | bytes 1474592 | tf_op jit(solution)/shard_map/all_to_all | solution.py:220
  281.4 4.9 %fusion.5 = f32[256,720]{0,1:T(8,128)} fusion(bf16[1,2880,720]{1,2,0:T(8,128)(2,1)} %param.32, bf16[32,8,2880]{2,1,0:T(8,128)(2,1)} %all-to-all-done, f32[720]{0:T(1024)S(1)} %reduce.2), kind=kOutput, calls=%fused_computation.22 | convolution fusion | flops 1061867520 | bytes 6361920 | tf_op jit(solution)/shard_map/dot_general | solution.py:129
  286.3 2.1 slice.39
  288.4 2.1 slice.40
  290.8 2.1 convolution_convert_fusion
  292.9 20.3 %copy.58 = bf16[32,8,2880]{1,0,2:T(8,128)(2,1)} copy(bf16[32,8,2880]{2,1,0:T(8,128)(2,1)} %convolution_convert_fusion) | data formatting | bytes 2949120
  313.2 32.7 %reshape.632 = bf16[2880,256]{1,0:T(8,128)(2,1)} reshape(bf16[2880,32,8]{2,1,0:T(8,128)(2,1)} %bitcast.95) | data formatting | bytes 2949120
  346.4 0.9 constant_dynamic-slice_fusion.1
  347.3 0.8 gather_fusion.7
  348.4 29.2 %reduce-scatter.4.cloned.1.call-done = bf16[360,256]{1,0:T(8,128)(2,1)} async-done(((bf16[2880,256]{1,0:T(8,128)(2,1)}), bf16[360,256]{1,0:T(8,128)(2,1)}) %reduce-scatter.4.cloned.1.call-update) | async-done | bytes 184336
  377.6 5.4 %reshape.633 = bf16[360,32,8]{2,1,0:T(8,128)(2,1)} reshape(bf16[360,256]{1,0:T(8,128)(2,1)} %reduce-scatter.4.cloned.1.call-done) | data formatting | bytes 368640
  382.9 4.5 %copy.59 = bf16[32,8,360]{2,1,0:T(8,128)(2,1)} copy(bf16[32,8,360]{1,0,2:T(8,128)(2,1)} %bitcast.100) | data formatting | bytes 368640
  387.4 10.1 %all-to-all-start.1 = ((bf16[32,8,360]{2,1,0:T(8,128)(2,1)}), bf16[32,8,360]{2,1,0:T(8,128)(2,1)S(1)}, u32[]{:S(2)}, u32[]{:S(2)}) async-start(bf16[32,8,360]{2,1,0:T(8,128)(2,1)} %copy.59), calls=%async_computation.1 | async-start | bytes 393216 | tf_op jit(solution)/shard_map/all_to_all | solution.py:230
  397.8 10.2 %all-to-all-done.1 = bf16[32,8,360]{2,1,0:T(8,128)(2,1)S(1)} async-done(((bf16[32,8,360]{2,1,0:T(8,128)(2,1)}), bf16[32,8,360]{2,1,0:T(8,128)(2,1)S(1)}, u32[]{:S(2)}, u32[]{:S(2)}) %all-to-all-start.1) | async-done | bytes 184352 | tf_op jit(solution)/shard_map/all_to_all | solution.py:230
  408.1 0.8 gather_fusion.6
  (149 shorter events, 20.0 us)
Async XLA Ops:
  6.5 284.2 %copy-start = (bf16[1,360,2880]{2,1,0:T(8,128)(2,1)S(1)}, bf16[1,360,2880]{2,1,0:T(8,128)(2,1)}, u32[]{:S(2)}) copy-start(bf16[1,360,2880]{2,1,0:T(8,128)(2,1)} %param.34) | copy-start | bytes 6220804
  6.5 85.2 %all-gather.11.cloned.1.call-start = ((), (), s32[]{:S(2)}) async-start(), calls=%async_computation.5 | async-start | bytes 3244032 | tf_op jit(solution)/shard_map/all_gather | solution.py:165
  7.3 165.6 %all-gather.9.cloned.1.call-start = ((), (), s32[]{:S(2)}) async-start(), calls=%async_computation.4 | async-start | bytes 4055040 | tf_op jit(solution)/shard_map/all_gather | solution.py:164
  8.0 216.5 %all-gather.7.cloned.1.call-start = ((), (), s32[]{:S(2)}) async-start(), calls=%async_computation.3 | async-start | bytes 1695744 | tf_op jit(solution)/shard_map/all_gather | solution.py:197
  36.3 5.7 %copy-start.3 = (bf16[32,2880]{1,0:T(8,128)(2,1)S(1)}, bf16[32,2880]{1,0:T(8,128)(2,1)}, u32[]{:S(2)}) copy-start(bf16[32,2880]{1,0:T(8,128)(2,1)} %param.18) | copy-start | bytes 552964
  36.3 6.5 %copy-start.2 = (s32[32]{0:T(128)S(1)}, s32[32]{0:T(128)}, u32[]{:S(2)}) copy-start(s32[32]{0:T(128)} %param.19) | copy-start | bytes 388
  96.1 81.6 %copy-start.8 = (f32[2880]{0:T(1024)S(1)}, f32[2880]{0:T(1024)}, u32[]{:S(2)}) copy-start(f32[2880]{0:T(1024)} %param.22) | copy-start | bytes 34564
  96.1 81.6 %copy-start.9 = (f32[640]{0:T(1024)S(1)}, f32[640]{0:T(1024)}, u32[]{:S(2)}) copy-start(f32[640]{0:T(1024)} %param.24) | copy-start | bytes 7684
  180.6 4.0 copy-start.11
  195.4 4.9 %copy-start.5 = (s32[32,4]{0,1:T(4,128)S(1)}, s32[32,4]{0,1:T(4,128)}, u32[]{:S(2)}) copy-start(s32[32,4]{0,1:T(4,128)} %param.31) | copy-start | bytes 1540
  196.6 29.6 %copy-start.7 = (f32[2880]{0:T(1024)S(1)}, f32[2880]{0:T(1024)}, u32[]{:S(2)}) copy-start(f32[2880]{0:T(1024)} %param.27) | copy-start | bytes 34564
  196.8 29.6 %copy-start.6 = (f32[2880]{0:T(1024)S(1)}, f32[2880]{0:T(1024)}, u32[]{:S(2)}) copy-start(f32[2880]{0:T(1024)} %param.28) | copy-start | bytes 34564
  230.9 12.9 %copy-start.10 = (f32[1,720]{1,0:T(1,128)S(1)}, f32[1,720]{1,0:T(1,128)}, u32[]{:S(2)}) copy-start(f32[1,720]{1,0:T(1,128)} %param.33) | copy-start | bytes 8644
  233.5 47.9 %all-to-all-start = ((bf16[32,8,2880]{2,1,0:T(8,128)(2,1)}), bf16[32,8,2880]{2,1,0:T(8,128)(2,1)}, u32[]{:S(2)}, u32[]{:S(2)}) async-start(bf16[32,8,2880]{2,1,0:T(8,128)(2,1)} %bitcast.101), calls=%async_computation | async-start | bytes 3014656 | tf_op jit(solution)/shard_map/all_to_all | solution.py:220
  243.6 134.0 %reduce-scatter.4.cloned.1.call-start = ((), (), s32[]{:S(2)}) async-start(), calls=%async_computation.6 | async-start | bytes 1658880
  345.9 2.2 copy-start.4
  345.9 2.2 copy-start.12
  382.9 27.0 %copy-start.1 = (bf16[1,360,2880]{2,1,0:T(8,128)(2,1)S(1)}, bf16[1,360,2880]{2,1,0:T(8,128)(2,1)}, u32[]{:S(2)}) copy-start(bf16[1,360,2880]{2,1,0:T(8,128)(2,1)} %param.34) | copy-start | bytes 6220804
  387.4 20.6 %all-to-all-start.1 = ((bf16[32,8,360]{2,1,0:T(8,128)(2,1)}), bf16[32,8,360]{2,1,0:T(8,128)(2,1)S(1)}, u32[]{:S(2)}, u32[]{:S(2)}) async-start(bf16[32,8,360]{2,1,0:T(8,128)(2,1)} %copy.59), calls=%async_computation.1 | async-start | bytes 393216 | tf_op jit(solution)/shard_map/all_to_all | solution.py:230
Sparse Core Ops, SparseCore 0:
  9.9 81.7 all-gather.10
  94.3 78.5 all-gather.8
  200.4 24.0 all-gather.6
  346.1 31.4 reduce-scatter.3
